TPU v7x, 256 devices: a whole 4x4x8 slice. The times are simulated.
256 devices in a mesh: role: 2 (over z_hi), dp: 16 (over y, z_lo), mp: 8 (over x, core).
Axes of the slice: x: 4, y: 4, z: 8 (z_hi: 2, z_lo: 4; z = z_hi * 4 + z_lo), core: 2. Of those that a mesh axis runs over, the one named last changes fastest.
Arguments:
- patches: bfloat16 [25088, 1280], P('dp', 'mp'), may hold values from -6 to 6
- pred_states: bfloat16 [16384, 384], P('dp'), may hold values from -6 to 6
- ema_up: bfloat16 [1280, 5120], P(('role', 'dp'), 'mp'), may hold values from -0.15625 to 0.15625
- ema_down: bfloat16 [5120, 1280], P('mp', ('role', 'dp')), may hold values from -0.078125 to 0.078125
- pred_up: bfloat16 [384, 1536], P(('role', 'dp'), 'mp'), may hold values from -0.3125 to 0.3125
- pred_down: bfloat16 [1536, 384], P('mp', ('role', 'dp')), may hold values from -0.15625 to 0.15625
- pred_out: bfloat16 [384, 1280], P(('role', 'dp'), 'mp'), may hold values from -0.3125 to 0.3125
- masked_index: int32 [16, 1024], P('dp'), may hold values from 0 to 1567, as said below
- masked_count: int32 [16], P('dp'), may hold values from 512 to 1024, as said below
- loss_scale: float32 [], replicated, may hold values from 81920 to 327680
Outputs:
- loss: float32 [], replicated
- grad_up: float32 [384, 1536], P(('role', 'dp'), 'mp')
- grad_down: float32 [1536, 384], P('mp', ('role', 'dp'))
- grad_out: float32 [384, 1280], P(('role', 'dp'), 'mp')
Inputs may be any that keep to these rules, and one draw needn't show every extreme that they name: `masked_index`: within a clip the slots name distinct tokens; the slots below masked_count name the masked tokens, which are whole tubes: all 8 frames (token f * 196 + s for frame f) of some spatial positions s. Slots from masked_count on name other tokens and are ignored. `masked_count`: each count is 8 times a whole number; some clip has exactly 1024.
All inputs are finite; a program needn't handle non-finite values.
Results may differ from a plain program's by a relative error of at most 0.012.
Values may be sent and summed in bfloat16 or wider, within the bound.
No kernel may reach another device: no remote copies, remote signals or barrier semaphores. Data moves between devices by JAX's collectives and lax.ppermute only.
A program may use at most 128 MiB of HBM per device.

v0:
```python
import functools
import jax
import jax.numpy as jnp
from jax import lax
from jax.sharding import Mesh
from jax.sharding import PartitionSpec as P

D = 1280
TOK = 1568
MMAX = 1024
MP = ("mp_0", "mp_1")
ROLE_DP = ("role", "dp_0", "dp_1")
DP = ("dp_0", "dp_1")
ROLE_DP_MP = ("role", "dp_0", "dp_1", "mp_0", "mp_1")
EPS = 1e-06
COEF = 0.7978845608028654


def joined_along(pieces, dim):
    pieces = jnp.moveaxis(pieces, 0, dim)
    lengths = pieces.shape
    return pieces.reshape(*lengths[:dim], lengths[dim] * lengths[dim + 1], *lengths[dim + 2 :])


def from_everyone(shard, axis):
    copies = jnp.broadcast_to(shard, (lax.axis_size(axis), *shard.shape))
    return lax.all_to_all(copies, axis, split_axis=0, concat_axis=0, tiled=True)


def gather_directly(shard, axis, dim):
    return joined_along(from_everyone(shard, axis), dim)


def of_everyone(shard, axis):
    return from_everyone(shard, axis).sum(axis=0)


def in_one(arrays, axis):
    vector, at, outs = (jnp.concatenate([a.reshape(-1) for a in arrays]), 0, [])
    total = of_everyone(vector, axis)
    for a in arrays:
        outs.append(total[at : at + a.size].reshape(a.shape))
        at += a.size
    return tuple(outs)


def passed_along(block, axis, distance):
    devices = range(lax.axis_size(axis))
    route = [(i - distance, i) for i in devices if i - distance in devices]
    return lax.ppermute(block, axis, route)


def sent_together(arrays, axis, dim, along):
    widths = [a.shape[along] for a in arrays]
    both = jnp.concatenate(arrays, axis=along)
    filled = lax.all_gather(both, axis, axis=dim, tiled=True)
    return tuple(jnp.split(filled, [sum(widths[:k]) for k in range(1, len(widths))], axis=along))


def by_axis(shard, axes):
    return functools.reduce(lax.psum, axes, shard)


def filled_up(lines, devices):
    spare = -len(lines) % devices
    return jnp.pad(lines, [(0, spare)] + [(0, 0)] * (lines.ndim - 1))


def sum_by_parts(shard, axis):
    lines = shard.reshape(-1, *shard.shape[1:][-1:])
    own = lax.psum_scatter(
        filled_up(lines, lax.axis_size(axis)), axis, scatter_dimension=0, tiled=True
    )
    whole = lax.all_gather(own, axis).reshape(-1, *lines.shape[1:])
    return lax.slice_in_dim(whole, 0, len(lines)).reshape(shard.shape)


def cut_along(shard, dim, devices):
    before, after = (shard.shape[:dim], shard.shape[dim + 1 :])
    return jnp.moveaxis(shard.reshape(*before, devices, -1, *after), dim, 0)


def sum_together(arrays, axis, dims):
    devices = lax.axis_size(axis)
    pieces = [cut_along(a, dim, devices) for a, dim in zip(arrays, dims)]
    lines = jnp.concatenate([b.reshape(devices, -1) for b in pieces], axis=1)
    width = max(16, -(-lines.shape[1] // 1024) * 8)
    lines = jnp.pad(lines, ((0, 0), (0, width * 128 - lines.shape[1]))).reshape(-1, 128)
    vector, at, outs = (lax.psum_scatter(lines, axis, tiled=True).reshape(-1), 0, [])
    for b in pieces:
        part = b[0]
        outs.append(vector[at : at + part.size].reshape(part.shape))
        at += part.size
    return tuple(outs)


def summed_on_arrival(shard, axis, dim):
    pieces = cut_along(shard, dim, lax.axis_size(axis))
    arrived = lax.all_to_all(pieces, axis, split_axis=0, concat_axis=0, tiled=True)
    return arrived.sum(axis=0)


def normalize(values):
    row_mean = jnp.mean(values, axis=-1, keepdims=True)
    row_deviations = values - row_mean
    variance = jnp.mean(row_deviations * row_deviations, axis=-1, keepdims=True)
    return row_deviations * lax.rsqrt(variance + EPS)


def gelu_slope(values):
    inner = COEF * (values + 0.044715 * values * values * values)
    tangent = jnp.tanh(inner)
    return 0.5 * (1.0 + tangent) + 0.5 * values * (1.0 - tangent * tangent) * COEF * (
        1.0 + 3.0 * 0.044715 * values * values
    )


def pick_rows(source_table, token_index):
    clip_count = token_index.shape[0]
    slot_total = token_index.shape[1]
    clip_grid = source_table.reshape(clip_count, TOK, source_table.shape[1])
    onehot = (token_index[:, :, None] == jnp.arange(TOK, dtype=jnp.int32)[None, None, :]).astype(
        jnp.bfloat16
    )
    picked = jnp.einsum("ckt,ctw->ckw", onehot, clip_grid, preferred_element_type=jnp.float32)
    return picked.astype(jnp.bfloat16).reshape(clip_count * slot_total, source_table.shape[1])


def body(
    patches,
    pred_states,
    ema_up,
    ema_down,
    pred_up,
    pred_down,
    pred_out,
    masked_index,
    masked_count,
    loss_scale,
):
    role_index = lax.axis_index("role")
    clip_count = masked_index.shape[0]
    feat_width = float(D)
    half_slots = MMAX // 2
    half_index = lax.dynamic_slice_in_dim(masked_index, role_index * half_slots, half_slots, 1)
    own_rows = pick_rows(patches, half_index)
    whole_rows = gather_directly(own_rows, MP, 1)
    working = role_index >= 0
    block_rows = own_rows.shape[0]
    up_cols = lax.all_gather(ema_up, ROLE_DP, axis=0, tiled=True)
    down_rows = lax.all_gather(ema_down, ROLE_DP, axis=1, tiled=True)

    def encode_block():
        normed = normalize(whole_rows.astype(jnp.float32)).astype(jnp.bfloat16)
        hidden = jax.nn.gelu(
            jnp.dot(normed, up_cols, preferred_element_type=jnp.float32), approximate=True
        ).astype(jnp.bfloat16)
        return jnp.dot(hidden, down_rows, preferred_element_type=jnp.float32)

    def skip_block():
        return jnp.zeros((block_rows, whole_rows.shape[1]), jnp.float32)

    partial_sum = lax.cond(working, encode_block, skip_block)
    branch = lax.psum_scatter(partial_sum, MP, scatter_dimension=1, tiled=True)
    block_out = own_rows.astype(jnp.float32) + branch
    first_sum, second_sum = in_one(
        (
            jnp.sum(block_out, axis=-1, keepdims=True),
            jnp.sum(block_out * block_out, axis=-1, keepdims=True),
        ),
        MP,
    )
    row_mean = first_sum / feat_width
    row_deviations = block_out - row_mean
    variance = second_sum / feat_width - row_mean * row_mean
    target_all = (row_deviations * lax.rsqrt(variance + EPS)).astype(jnp.bfloat16)
    local_width = target_all.shape[1]
    earlier = passed_along(target_all, "role", 1)
    joined = jnp.concatenate(
        (
            earlier.reshape(clip_count, half_slots, local_width),
            target_all.reshape(clip_count, half_slots, local_width),
        ),
        axis=1,
    )
    targets = joined.reshape(clip_count * MMAX, local_width)
    up_rows, out_rows = sent_together((pred_up, pred_out), ROLE_DP, 0, 1)
    down_cols = gather_directly(pred_down, ROLE_DP, 1)
    total = of_everyone(jnp.sum(masked_count).astype(jnp.float32), DP)
    states = pred_states.astype(jnp.float32)
    pnormed = normalize(states).astype(jnp.bfloat16)
    preact = jnp.dot(pnormed, up_rows, preferred_element_type=jnp.float32)
    hid_act = jax.nn.gelu(preact, approximate=True).astype(jnp.bfloat16)
    mixer_out = lax.psum(jnp.dot(hid_act, down_cols, preferred_element_type=jnp.float32), MP)
    updated = states + mixer_out
    row_mean_p = jnp.mean(updated, axis=-1, keepdims=True)
    predictor_deviations = updated - row_mean_p
    reciprocal_spread = lax.rsqrt(
        jnp.mean(predictor_deviations * predictor_deviations, axis=-1, keepdims=True) + EPS
    )
    standardized_input = predictor_deviations * reciprocal_spread
    output_normalized = standardized_input.astype(jnp.bfloat16)
    predicted = jnp.dot(output_normalized, out_rows, preferred_element_type=jnp.float32)
    live_mask = (
        (jnp.arange(MMAX, dtype=jnp.int32)[None, :] < masked_count[:, None])
        .astype(jnp.float32)
        .reshape(clip_count * MMAX, 1)
    )
    predictor_side = (role_index == 1).astype(jnp.float32)
    norm_scale = total * feat_width
    residue = predicted - targets.astype(jnp.float32)
    smooth = jnp.sqrt(residue * residue + 1.0)
    local_loss = jnp.sum(live_mask * (smooth - 1.0)) * predictor_side
    loss = by_axis(local_loss, ROLE_DP_MP) / norm_scale
    grad_pred = (loss_scale * live_mask * residue / smooth / norm_scale * predictor_side).astype(
        jnp.bfloat16
    )
    normalized_gradient = sum_by_parts(
        jnp.einsum("rd,kd->rk", grad_pred, out_rows, preferred_element_type=jnp.float32), MP
    )
    gradient_update = reciprocal_spread * (
        normalized_gradient
        - jnp.mean(normalized_gradient, axis=-1, keepdims=True)
        - standardized_input
        * jnp.mean(normalized_gradient * standardized_input, axis=-1, keepdims=True)
    )
    gradient_update = gradient_update.astype(jnp.bfloat16)
    down_local = jnp.einsum(
        "rf,rk->fk", hid_act, gradient_update, preferred_element_type=jnp.float32
    )
    grad_act = jnp.einsum(
        "rk,fk->rf", gradient_update, down_cols, preferred_element_type=jnp.float32
    )
    grad_pre = (grad_act * gelu_slope(preact)).astype(jnp.bfloat16)
    up_local = jnp.einsum("rk,rf->kf", pnormed, grad_pre, preferred_element_type=jnp.float32)
    out_local = jnp.einsum(
        "rk,rd->kd", output_normalized, grad_pred, preferred_element_type=jnp.float32
    )
    grad_up, grad_out = tuple(
        (
            part.astype(jnp.float32)
            for part in sum_together(
                (up_local.astype(jnp.bfloat16), out_local.astype(jnp.bfloat16)), ROLE_DP, (0, 0)
            )
        )
    )
    grad_down = summed_on_arrival(down_local, ROLE_DP, 1)
    return (loss, grad_up, grad_down, grad_out)


def solution(mesh):
    finer = Mesh(
        mesh.devices.reshape(mesh.shape["role"], 4, 4, 4, 2),
        ("role", "dp_0", "dp_1", "mp_0", "mp_1"),
    )
    return jax.shard_map(
        body,
        mesh=finer,
        in_specs=(
            P(DP, MP),
            P(DP, None),
            P(ROLE_DP, MP),
            P(MP, ROLE_DP),
            P(ROLE_DP, MP),
            P(MP, ROLE_DP),
            P(ROLE_DP, MP),
            P(DP, None),
            P(DP),
            P(),
        ),
        out_specs=(P(), P(ROLE_DP, MP), P(MP, ROLE_DP), P(ROLE_DP, MP)),
        check_vma=False,
    )
```

profile of v0, /device:TPU:2, one launch (start us, length us, event | category | flops | bytes accessed | tf_op | source)
XLA Modules:
  0.0 619.0 jit_solution(12182839815354292576)
XLA Ops:
  10.9 11.5 %all-to-all-start = ((bf16[32,192,12]{1,2,0:T(8,128)(2,1)}), bf16[32,192,12]{1,2,0:T(8,128)(2,1)S(1)}, u32[]{:S(2)}, u32[]{:S(2)}) async-start(bf16[32,192,12]{1,2,0:T(8,128)(2,1)} %broadcast_in_dim.10), calls=%async_computation | async-start | bytes 524288 | tf_op jit(solution)/shard_map/all_to_all | solution.py:27
  23.2 75.8 %all-gather.1 = bf16[32,12,352]{2,1,0:T(8,128)(2,1)S(1)} all-gather(bf16[1,12,352]{2,1,0:T(8,128)(2,1)S(1)} %maximum_bitcast_fusion.1), channel_id=1, replica_groups=mesh['role'=2,'dp_0'=4,'dp_1'=4,'mp_0'=4,'mp_1'=2] {'role','dp_0','dp_1'}, dimensions={0}, use_global_device_ids=true | all-gather | bytes 278784 | tf_op jit(solution)/shard_map/all_gather | solution.py:56
  102.9 4.8 all-to-all-start.1
  107.7 1.6 fusion.61
  109.3 1.9 reshape.172
  111.2 2.6 fusion.79
  113.9 11.1 %all-to-all-done.1 = bf16[8,512,160]{1,2,0:T(8,128)(2,1)S(1)} async-done(((bf16[8,512,160]{1,2,0:T(8,128)(2,1)}), bf16[8,512,160]{1,2,0:T(8,128)(2,1)S(1)}, u32[]{:S(2)}, u32[]{:S(2)}) %all-to-all-start.1) | async-done | bytes 1310752 | tf_op jit(solution)/shard_map/all_to_all | solution.py:27
  124.9 32.0 %all-gather.6.cloned.1.call-done = bf16[1280,640]{1,0:T(8,128)(2,1)} async-done(((bf16[40,640]{1,0:T(8,128)(2,1)}), bf16[1280,640]{1,0:T(8,128)(2,1)}) %all-gather.6.cloned.1.call-update) | async-done | bytes 1638416 | tf_op jit(solution)/shard_map/all_gather | solution.py:150
  156.9 142.1 %all-gather.8.cloned.1.call-done = bf16[640,1280]{0,1:T(8,128)(2,1)} async-done(((bf16[640,40]{0,1:T(8,128)(2,1)}), bf16[640,1280]{0,1:T(8,128)(2,1)}) %all-gather.8.cloned.1.call-update) | async-done | bytes 1638416 | tf_op jit(solution)/shard_map/all_gather | solution.py:151
  299.0 8.5 %conditional.1 = (f32[512,1280]{1,0:T(8,128)}) conditional(s32[]{:T(128)} %convert_element_type.101, () %tuple.14, (bf16[512,8,160]{0,2,1:T(8,128)(2,1)S(1)}, bf16[1280,640]{1,0:T(8,128)(2,1)}, bf16[640,1280]{0,1:T(8,128)(2,1)}) %tuple.41), branch_computations={%region_5.0_spmd, %region_6.9_spmd} | conditional | flops 1687224832 | bytes 12470280 | solution.py:163
  301.1 6.4 %fusion.10 = f32[512,1280]{1,0:T(8,128)} fusion(bf16[640,1280]{0,1:T(8,128)(2,1)} %get-tuple-element.25, bf16[512,1280]{0,1:T(8,128)(2,1)} %fusion.1, bf16[1280,640]{1,0:T(8,128)(2,1)} %get-tuple-element.11), kind=kOutput, calls=%fused_computation.14 | convolution fusion | flops 1680670720 | bytes 7208960 | tf_op jit(solution)/shard_map/cond/branch_1_fun/dot_general | solution.py:158
  307.5 3.2 copy.34
  312.0 5.7 all-to-all-start.3
  318.4 7.2 %all-to-all-done.3 = f32[16,1,1]{2,1,0:T(1,128)S(1)} async-done(((f32[16,1,1]{2,1,0:T(1,128)}), f32[16,1,1]{2,1,0:T(1,128)S(1)}, u32[]{:S(2)}, u32[]{:S(2)}) %all-to-all-start.3) | async-done | bytes 96 | tf_op jit(solution)/shard_map/all_to_all | solution.py:27
  326.9 1.8 fusion.81
  329.3 13.2 %reduce-scatter.3.cloned.1.call-done = f32[512,160]{0,1:T(8,128)} async-done(((f32[512,1280]{0,1:T(8,128)}), f32[512,160]{0,1:T(8,128)}) %reduce-scatter.3.cloned.1.call-update) | async-done | bytes 327696 | tf_op jit(solution)/shard_map/reduce_scatter | solution.py:164
  344.2 7.0 %all-to-all-start.2 = ((f32[8,1,1024]{2,1,0:T(1,128)}), f32[8,1,1024]{2,1,0:T(1,128)S(1)}, u32[]{:S(2)}, u32[]{:S(2)}) async-start(f32[8,1,1024]{2,1,0:T(1,128)} %broadcast_in_dim.12), calls=%async_computation.3 | async-start | bytes 65536 | tf_op jit(solution)/shard_map/all_to_all | solution.py:27
  351.2 4.0 all-to-all-done.2
  356.3 7.8 %collective-permute-start = (bf16[512,160]{0,1:T(8,128)(2,1)S(1)}, bf16[512,160]{0,1:T(8,128)(2,1)S(1)}, u32[]{:S(2)}, u32[]{:S(2)}) collective-permute-start(bf16[512,160]{0,1:T(8,128)(2,1)S(1)} %multiply_convert_fusion.2), channel_id=1, source_target_pairs={{0,128},{1,129},{2,130},{3,131},{4,132},{5,133},{6,134},{7,135},{8... | collective-permute-start | bytes 491528 | tf_op jit(solution)/shard_map/ppermute | solution.py:50
  364.5 3.0 collective-permute-done
  369.0 1.7 fusion.63
  371.0 36.0 %reduce-scatter.5.cloned.1.call-done = f32[128,384]{1,0:T(8,128)} async-done(((f32[1024,384]{1,0:T(8,128)}), f32[128,384]{1,0:T(8,128)}) %reduce-scatter.5.cloned.1.call-update) | async-done | bytes 196624 | tf_op jit(solution)/shard_map/reduce_scatter | solution.py:71
  408.8 27.1 %all-gather.10.cloned.1.call-done = f32[1024,384]{1,0:T(8,128)} async-done(((f32[128,384]{1,0:T(8,128)}), f32[1024,384]{1,0:T(8,128)}) %all-gather.10.cloned.1.call-update) | async-done | bytes 1572880 | tf_op jit(solution)/shard_map/all_gather | solution.py:74
  436.0 2.2 multiply_reduce_fusion.1
  441.2 2.3 fusion.30
  444.4 10.0 %all-to-all-start.4 = ((f32[32,192,12]{1,2,0:T(8,128)}), f32[32,192,12]{1,2,0:T(8,128)S(1)}, u32[]{:S(2)}, u32[]{:S(2)}) async-start(f32[32,192,12]{1,2,0:T(8,128)} %bitcast.9), calls=%async_computation.6 | async-start | bytes 1048576 | tf_op jit(solution)/shard_map/all_to_all | solution.py:99
  456.4 16.2 %psum.43 = f32[]{:T(128)} all-reduce(f32[]{:T(128)S(6)} %mul.192), channel_id=1, replica_groups=mesh['role'=2,'dp_0'=4,'dp_1'=4,'mp_0'=4,'mp_1'=2] {'role'}, use_global_device_ids=true, to_apply=%region_14.0 | all-reduce | flops 1 | bytes 8 | tf_op jit(solution)/shard_map/psum | solution.py:61
  472.6 10.4 %psum.44 = f32[]{:T(128)} all-reduce(f32[]{:T(128)} %psum.43), channel_id=1, replica_groups=mesh['role'=2,'dp_0'=4,'dp_1'=4,'mp_0'=4,'mp_1'=2] {'dp_0'}, use_global_device_ids=true, to_apply=%region_15.0 | all-reduce | flops 1 | bytes 8 | tf_op jit(solution)/shard_map/psum | solution.py:61
  483.6 10.3 %psum.45 = f32[]{:T(128)} all-reduce(f32[]{:T(128)} %psum.44), channel_id=1, replica_groups=mesh['role'=2,'dp_0'=4,'dp_1'=4,'mp_0'=4,'mp_1'=2] {'dp_1'}, use_global_device_ids=true, to_apply=%region_16.0 | all-reduce | flops 1 | bytes 8 | tf_op jit(solution)/shard_map/psum | solution.py:61
  494.5 10.4 %psum.46 = f32[]{:T(128)} all-reduce(f32[]{:T(128)} %psum.45), channel_id=1, replica_groups=mesh['role'=2,'dp_0'=4,'dp_1'=4,'mp_0'=4,'mp_1'=2] {'mp_0'}, use_global_device_ids=true, to_apply=%region_17.0 | all-reduce | flops 1 | bytes 8 | tf_op jit(solution)/shard_map/psum | solution.py:61
  504.9 3.1 psum.47
  508.6 98.4 %all-reduce.7.cloned.1.call-done = bf16[1280,128]{1,0:T(8,128)(2,1)} async-done(((bf16[1280,128]{1,0:T(8,128)(2,1)}), bf16[1280,128]{1,0:T(8,128)(2,1)}) %all-reduce.7.cloned.1.call-update) | async-done | bytes 327696
  (96 shorter events, 27.4 us)
Async XLA Ops:
  8.0 92.6 %copy-start = (bf16[1568,160]{0,1:T(8,128)(2,1)S(1)}, bf16[1568,160]{0,1:T(8,128)(2,1)}, u32[]{:S(2)}) copy-start(bf16[1568,160]{0,1:T(8,128)(2,1)} %param.12) | copy-start | bytes 1505284
  8.0 91.0 %copy-start.1 = (bf16[1024,384]{1,0:T(8,128)(2,1)S(1)}, bf16[1024,384]{1,0:T(8,128)(2,1)}, u32[]{:S(2)}) copy-start(bf16[1024,384]{1,0:T(8,128)(2,1)} %param.13) | copy-start | bytes 2359300
  8.0 91.7 %copy-start.14 = (s32[1,1024]{1,0:T(1,128)S(1)}, s32[1,1024]{1,0:T(1,128)}, u32[]{:S(2)}) copy-start(s32[1,1024]{1,0:T(1,128)} %param.19) | copy-start | bytes 12292
  8.0 148.9 %all-gather.6.cloned.1.call-start = ((), (), s32[]{:S(2)}) async-start(), calls=%async_computation.8 | async-start | bytes 1689600 | tf_op jit(solution)/shard_map/all_gather | solution.py:150
  8.8 290.2 %all-gather.8.cloned.1.call-start = ((), (), s32[]{:S(2)}) async-start(), calls=%async_computation.9 | async-start | bytes 1689600 | tf_op jit(solution)/shard_map/all_gather | solution.py:151
  10.9 90.7 %all-to-all-start = ((bf16[32,192,12]{1,2,0:T(8,128)(2,1)}), bf16[32,192,12]{1,2,0:T(8,128)(2,1)S(1)}, u32[]{:S(2)}, u32[]{:S(2)}) async-start(bf16[32,192,12]{1,2,0:T(8,128)(2,1)} %broadcast_in_dim.10), calls=%async_computation | async-start | bytes 524288 | tf_op jit(solution)/shard_map/all_to_all | solution.py:27
  101.6 1.3 copy-start.9
  101.6 1.3 copy-start.11
  102.9 22.0 %all-to-all-start.1 = ((bf16[8,512,160]{1,2,0:T(8,128)(2,1)}), bf16[8,512,160]{1,2,0:T(8,128)(2,1)S(1)}, u32[]{:S(2)}, u32[]{:S(2)}) async-start(bf16[8,512,160]{1,2,0:T(8,128)(2,1)} %broadcast_in_dim.11), calls=%async_computation.1 | async-start | bytes 2621440 | tf_op jit(solution)/shard_map/all_to_all | solution.py:27
  107.7 219.2 %all-reduce.5.cloned.1.call-start = ((), (), s32[]{:S(2)}) async-start(), calls=%async_computation.7 | async-start | bytes 3145728 | tf_op jit(solution)/shard_map/psum | solution.py:194
  109.3 4.5 copy-start.4
  113.8 228.6 %reduce-scatter.3.cloned.1.call-start = ((), (), s32[]{:S(2)}) async-start(), calls=%async_computation.10 | async-start | bytes 2949120 | tf_op jit(solution)/shard_map/reduce_scatter | solution.py:164
  312.0 13.6 %all-to-all-start.3 = ((f32[16,1,1]{2,1,0:T(1,128)}), f32[16,1,1]{2,1,0:T(1,128)S(1)}, u32[]{:S(2)}, u32[]{:S(2)}) async-start(f32[16,1,1]{2,1,0:T(1,128)} %broadcast_in_dim.13), calls=%async_computation.4 | async-start | bytes 16384 | tf_op jit(solution)/shard_map/all_to_all | solution.py:27
  326.8 1.9 copy-start.2
  328.7 13.8 %copy-start.10 = (bf16[512,160]{0,1:T(8,128)(2,1)S(1)}, bf16[512,160]{0,1:T(8,128)(2,1)}, u32[]{:S(2)}) copy-start(bf16[512,160]{0,1:T(8,128)(2,1)} %copy-done.9) | copy-start | bytes 491524
  344.2 11.1 %all-to-all-start.2 = ((f32[8,1,1024]{2,1,0:T(1,128)}), f32[8,1,1024]{2,1,0:T(1,128)S(1)}, u32[]{:S(2)}, u32[]{:S(2)}) async-start(f32[8,1,1024]{2,1,0:T(1,128)} %broadcast_in_dim.12), calls=%async_computation.3 | async-start | bytes 65536 | tf_op jit(solution)/shard_map/all_to_all | solution.py:27
  351.2 55.7 %reduce-scatter.5.cloned.1.call-start = ((), (), s32[]{:S(2)}) async-start(), calls=%async_computation.11 | async-start | bytes 1769472 | tf_op jit(solution)/shard_map/reduce_scatter | solution.py:71
  356.3 11.2 %copy-start.8 = (bf16[384,352]{1,0:T(8,128)(2,1)S(1)}, bf16[384,352]{1,0:T(8,128)(2,1)}, u32[]{:S(2)}) copy-start(bf16[384,352]{1,0:T(8,128)(2,1)} %reshape.189) | copy-start | bytes 811012
  356.3 11.1 %collective-permute-start = (bf16[512,160]{0,1:T(8,128)(2,1)S(1)}, bf16[512,160]{0,1:T(8,128)(2,1)S(1)}, u32[]{:S(2)}, u32[]{:S(2)}) collective-permute-start(bf16[512,160]{0,1:T(8,128)(2,1)S(1)} %multiply_convert_fusion.2), channel_id=1, source_target_pairs={{0,128},{1,129},{2,130},{3,131},{4,132},{5,133},{6,134},{7,135},{8... | collective-permute-start | bytes 491528 | tf_op jit(solution)/shard_map/ppermute | solution.py:50
  364.5 4.5 copy-start.7
  370.7 65.2 %all-gather.10.cloned.1.call-start = ((), (), s32[]{:S(2)}) async-start(), calls=%async_computation.12 | async-start | bytes 1769472 | tf_op jit(solution)/shard_map/all_gather | solution.py:74
  436.0 2.3 copy-start.3
  438.2 1.8 copy-start.5
  439.2 0.9 copy-start.12
  440.1 1.1 copy-start.6
  440.1 1.2 copy-start.13
  444.4 38.6 %copy-start.15 = (u32[256]{0:T(256)S(1)}, u32[256]{0:T(256)}, u32[]{:S(2)}) copy-start(u32[256]{0:T(256)} %constant.79) | copy-start | bytes 3076
  444.4 165.4 %all-to-all-start.4 = ((f32[32,192,12]{1,2,0:T(8,128)}), f32[32,192,12]{1,2,0:T(8,128)S(1)}, u32[]{:S(2)}, u32[]{:S(2)}) async-start(f32[32,192,12]{1,2,0:T(8,128)} %bitcast.9), calls=%async_computation.6 | async-start | bytes 1048576 | tf_op jit(solution)/shard_map/all_to_all | solution.py:99
  454.4 152.7 %all-reduce.7.cloned.1.call-start = ((), (), s32[]{:S(2)}) async-start(), calls=%async_computation.13 | async-start | bytes 655360
Sparse Core Ops, SparseCore 0:
  10.6 146.2 all-gather.5
  158.7 140.2 all-gather.7
  458.6 148.3 all-reduce.6
Sparse Core Ops, SparseCore 1:
  113.9 67.6 all-reduce.4
  310.8 31.6 reduce-scatter.2
  370.8 36.1 reduce-scatter.4
  408.8 27.1 all-gather.9
where the time goes:
time: 620 us; the launch traced here: 619 us
  waiting for transfers between devices  375 us (60%)
  blocking collectives  126 us (20%)
  starting transfers between devices  47.1 us (8%)
  between operations  20.9 us (3%)
  matrix products  19.1 us (3%)
  local copies, waits for them, and re-layouts  15.9 us (3%)
  other arithmetic  14.2 us (2%)
    all_gather x1, waiting for transfers between devices, body(): down_rows = lax.all_gather(ema_down, ROLE_DP, axis=1, tiled=True)  142 us
    unnamed x8, waiting for transfers between devices  99.9 us
    all_gather x1, blocking collectives, sent_together(): filled = lax.all_gather(both, axis, axis=dim, tiled=True)  75.8 us
    psum x5, blocking collectives, by_axis(): return functools.reduce(lax.psum, axes, shard)  50.4 us
    reduce_scatter x1, waiting for transfers between devices, sum_by_parts(): lax.psum_scatter(filled_up(lines, lax.axis_size(axis)), axis, scatter_dim...  36 us
    all_gather x1, waiting for transfers between devices, body(): up_cols = lax.all_gather(ema_up, ROLE_DP, axis=0, tiled=True)  32 us
    all_to_all x4, starting transfers between devices, from_everyone(): return lax.all_to_all(copies, axis, split_axis=0, concat_axis=0, tiled=True)  29 us
    all_gather x1, waiting for transfers between devices, sum_by_parts(): whole = lax.all_gather(own, axis).reshape(-1, *lines.shape[1:])  27.1 us
  transfers between devices with their start and end apart: 13, of which 10 were waited for; matrix products, arithmetic and copies ran while one was open for 6% of the time, Pallas kernels for 0%

commit v1 on v0

--- a/solution.py
+++ b/solution.py
@@ -147,7 +147,9 @@
     whole_rows = gather_directly(own_rows, MP, 1)
     working = role_index >= 0
     block_rows = own_rows.shape[0]
-    up_cols = lax.all_gather(ema_up, ROLE_DP, axis=0, tiled=True)
+    up_cols = jnp.concatenate(
+        lax.all_to_all(jnp.stack([ema_up] * lax.axis_size(ROLE_DP)), ROLE_DP, 0, 0), axis=0
+    )
     down_rows = lax.all_gather(ema_down, ROLE_DP, axis=1, tiled=True)
 
     def encode_block():

time: 620 us -> 566 us (0.913)
  waiting for transfers between devices: 375 us -> 280 us
  blocking collectives: 126 us -> 164 us
    all_gather x1, waiting for transfers between devices: 142 us -> 4.71 us  [body(): down_rows = lax.all_gather(ema_down, ROLE_DP, axis=1, tiled=True)]
    all_gather x1, blocking collectives: 75.8 us -> 113 us  [sent_together(): filled = lax.all_gather(both, axis, axis=dim, tiled=True)]
    psum x1, waiting for transfers between devices: 0.03 us -> 34.8 us  [body(): lax.psum(jnp.dot(hid_act, down_cols, preferred_element_type=jnp.float32),...]
    all_gather x1 -> x0, waiting for transfers between devices: 32 us -> none  [body(): up_cols = lax.all_gather(ema_up, ROLE_DP, axis=0, tiled=True)]
    reduce_scatter x1, waiting for transfers between devices: 13.2 us -> 35.9 us  [body(): branch = lax.psum_scatter(partial_sum, MP, scatter_dimension=1, tiled=True)]
    all_to_all x4, waiting for transfers between devices: 22.2 us -> 39.6 us  [from_everyone(): return lax.all_to_all(copies, axis, split_axis=0, concat_axis=0, tiled=True)]
    unnamed x8 -> x7, waiting for transfers between devices: 99.9 us -> 99.2 us
  transfers between devices with their start and end apart: 13 -> 13, of which waited for: 10 -> 11; matrix products, arithmetic and copies ran while one was open for 6% -> 6% of each run, Pallas kernels for 0% -> 0%
where the time goes in v1:
time: 566 us; the launch traced here: 565 us
  waiting for transfers between devices  280 us (49%)
  blocking collectives  164 us (29%)
  starting transfers between devices  50 us (9%)
  between operations  21.1 us (4%)
  local copies, waits for them, and re-layouts  18.2 us (3%)
  matrix products  18.2 us (3%)
  other arithmetic  13.5 us (2%)
    all_gather x1, blocking collectives, sent_together(): filled = lax.all_gather(both, axis, axis=dim, tiled=True)  113 us
    unnamed x7, waiting for transfers between devices  99.2 us
    psum x5, blocking collectives, by_axis(): return functools.reduce(lax.psum, axes, shard)  50.4 us
    all_to_all x4, waiting for transfers between devices, from_everyone(): return lax.all_to_all(copies, axis, split_axis=0, concat_axis=0, tiled=True)  39.6 us
    reduce_scatter x1, waiting for transfers between devices, sum_by_parts(): lax.psum_scatter(filled_up(lines, lax.axis_size(axis)), axis, scatter_dim...  35.9 us
    reduce_scatter x1, waiting for transfers between devices, body(): branch = lax.psum_scatter(partial_sum, MP, scatter_dimension=1, tiled=True)  35.9 us
    psum x1, waiting for transfers between devices, body(): lax.psum(jnp.dot(hid_act, down_cols, preferred_element_type=jnp.float32),...  34.8 us
    all_gather x1, waiting for transfers between devices, sum_by_parts(): whole = lax.all_gather(own, axis).reshape(-1, *lines.shape[1:])  27.1 us
  transfers between devices with their start and end apart: 13, of which 11 were waited for; matrix products, arithmetic and copies ran while one was open for 6% of the time, Pallas kernels for 0%

profile of v1, /device:TPU:2, one launch (start us, length us, event | category | flops | bytes accessed | tf_op | source)
XLA Modules:
  0.0 565.0 jit_solution(5718748929242099711)
XLA Ops:
  9.5 11.5 %all-to-all-start = ((bf16[32,192,12]{1,2,0:T(8,128)(2,1)}), bf16[32,192,12]{1,2,0:T(8,128)(2,1)S(1)}, u32[]{:S(2)}, u32[]{:S(2)}) async-start(bf16[32,192,12]{1,2,0:T(8,128)(2,1)} %broadcast_in_dim.10), calls=%async_computation | async-start | bytes 524288 | tf_op jit(solution)/shard_map/all_to_all | solution.py:27
  22.6 12.0 %all-to-all-done = bf16[32,192,12]{1,2,0:T(8,128)(2,1)S(1)} async-done(((bf16[32,192,12]{1,2,0:T(8,128)(2,1)}), bf16[32,192,12]{1,2,0:T(8,128)(2,1)S(1)}, u32[]{:S(2)}, u32[]{:S(2)}) %all-to-all-start) | async-done | bytes 147488 | tf_op jit(solution)/shard_map/all_to_all | solution.py:27
  35.8 5.0 all-to-all-start.1
  41.5 16.6 %all-to-all-done.1 = bf16[8,512,160]{1,2,0:T(8,128)(2,1)S(1)} async-done(((bf16[8,512,160]{1,2,0:T(8,128)(2,1)}), bf16[8,512,160]{1,2,0:T(8,128)(2,1)S(1)}, u32[]{:S(2)}, u32[]{:S(2)}) %all-to-all-start.1) | async-done | bytes 1310752 | tf_op jit(solution)/shard_map/all_to_all | solution.py:27
  59.4 4.8 all-to-all-start.2
  64.4 113.4 %all-gather.1 = bf16[32,12,352]{2,1,0:T(8,128)(2,1)S(1)} all-gather(bf16[1,12,352]{2,1,0:T(8,128)(2,1)S(1)} %maximum_bitcast_fusion.1), channel_id=1, replica_groups=mesh['role'=2,'dp_0'=4,'dp_1'=4,'mp_0'=4,'mp_1'=2] {'role','dp_0','dp_1'}, dimensions={0}, use_global_device_ids=true | all-gather | bytes 278784 | tf_op jit(solution)/shard_map/all_gather | solution.py:56
  180.3 1.9 reshape.185
  182.2 2.6 fusion.81
  184.9 4.7 all-gather.5.cloned.1.call-done
  189.6 8.5 %conditional.1 = (f32[512,1280]{1,0:T(8,128)}) conditional(s32[]{:T(128)} %convert_element_type.100, () %tuple.14, (bf16[512,8,160]{0,2,1:T(8,128)(2,1)S(1)}, bf16[32,40,640]{2,1,0:T(8,128)(2,1)}, bf16[640,1280]{0,1:T(8,128)(2,1)}) %tuple.39), branch_computations={%region_5.0_spmd, %region_6.9_spmd} | conditional | flops 1687224832 | bytes 12470280 | solution.py:165
  191.7 6.4 %fusion.12 = f32[512,1280]{1,0:T(8,128)} fusion(bf16[640,1280]{0,1:T(8,128)(2,1)} %get-tuple-element.26, bf16[512,1280]{0,1:T(8,128)(2,1)} %bitcast.39, bf16[1280,640]{1,0:T(8,128)(2,1)} %bitcast.1), kind=kOutput, calls=%fused_computation.15 | convolution fusion | flops 1680670720 | bytes 7208960 | tf_op jit(solution)/shard_map/cond/branch_1_fun/dot_general | solution.py:160
  198.1 3.2 copy.34
  202.7 3.5 all-to-all-start.4
  206.8 7.1 %all-to-all-done.4 = f32[16,1,1]{2,1,0:T(1,128)S(1)} async-done(((f32[16,1,1]{2,1,0:T(1,128)}), f32[16,1,1]{2,1,0:T(1,128)S(1)}, u32[]{:S(2)}, u32[]{:S(2)}) %all-to-all-start.4) | async-done | bytes 96 | tf_op jit(solution)/shard_map/all_to_all | solution.py:27
  215.2 34.8 %all-reduce.5.cloned.1.call-done = f32[1024,384]{1,0:T(8,128)} async-done(((f32[1024,384]{1,0:T(8,128)}), f32[1024,384]{1,0:T(8,128)}) %all-reduce.5.cloned.1.call-update) | async-done | bytes 1572880 | tf_op jit(solution)/shard_map/psum | solution.py:196
  250.0 1.8 fusion.83
  252.4 35.9 %reduce-scatter.3.cloned.1.call-done = f32[512,160]{0,1:T(8,128)} async-done(((f32[512,1280]{0,1:T(8,128)}), f32[512,160]{0,1:T(8,128)}) %reduce-scatter.3.cloned.1.call-update) | async-done | bytes 327696 | tf_op jit(solution)/shard_map/reduce_scatter | solution.py:166
  290.0 7.1 %all-to-all-start.3 = ((f32[8,1,1024]{2,1,0:T(1,128)}), f32[8,1,1024]{2,1,0:T(1,128)S(1)}, u32[]{:S(2)}, u32[]{:S(2)}) async-start(f32[8,1,1024]{2,1,0:T(1,128)} %broadcast_in_dim.12), calls=%async_computation.4 | async-start | bytes 65536 | tf_op jit(solution)/shard_map/all_to_all | solution.py:27
  297.1 4.0 all-to-all-done.3
  302.2 7.8 %collective-permute-start = (bf16[512,160]{0,1:T(8,128)(2,1)S(1)}, bf16[512,160]{0,1:T(8,128)(2,1)S(1)}, u32[]{:S(2)}, u32[]{:S(2)}) collective-permute-start(bf16[512,160]{0,1:T(8,128)(2,1)S(1)} %multiply_convert_fusion.2), channel_id=1, source_target_pairs={{0,128},{1,129},{2,130},{3,131},{4,132},{5,133},{6,134},{7,135},{8... | collective-permute-start | bytes 491528 | tf_op jit(solution)/shard_map/ppermute | solution.py:50
  310.3 3.0 collective-permute-done
  316.8 35.9 %reduce-scatter.5.cloned.1.call-done = f32[128,384]{1,0:T(8,128)} async-done(((f32[1024,384]{1,0:T(8,128)}), f32[128,384]{1,0:T(8,128)}) %reduce-scatter.5.cloned.1.call-update) | async-done | bytes 196624 | tf_op jit(solution)/shard_map/reduce_scatter | solution.py:71
  354.6 27.1 %all-gather.7.cloned.1.call-done = f32[1024,384]{1,0:T(8,128)} async-done(((f32[128,384]{1,0:T(8,128)}), f32[1024,384]{1,0:T(8,128)}) %all-gather.7.cloned.1.call-update) | async-done | bytes 1572880 | tf_op jit(solution)/shard_map/all_gather | solution.py:74
  381.8 2.2 multiply_reduce_fusion
  387.0 2.3 fusion.32
  390.2 10.0 %all-to-all-start.5 = ((f32[32,192,12]{1,2,0:T(8,128)}), f32[32,192,12]{1,2,0:T(8,128)S(1)}, u32[]{:S(2)}, u32[]{:S(2)}) async-start(f32[32,192,12]{1,2,0:T(8,128)} %bitcast.10), calls=%async_computation.7 | async-start | bytes 1048576 | tf_op jit(solution)/shard_map/all_to_all | solution.py:99
  402.1 16.2 %psum.43 = f32[]{:T(128)} all-reduce(f32[]{:T(128)S(6)} %mul.193), channel_id=1, replica_groups=mesh['role'=2,'dp_0'=4,'dp_1'=4,'mp_0'=4,'mp_1'=2] {'role'}, use_global_device_ids=true, to_apply=%region_14.0 | all-reduce | flops 1 | bytes 8 | tf_op jit(solution)/shard_map/psum | solution.py:61
  418.4 10.4 %psum.44 = f32[]{:T(128)} all-reduce(f32[]{:T(128)} %psum.43), channel_id=1, replica_groups=mesh['role'=2,'dp_0'=4,'dp_1'=4,'mp_0'=4,'mp_1'=2] {'dp_0'}, use_global_device_ids=true, to_apply=%region_15.0 | all-reduce | flops 1 | bytes 8 | tf_op jit(solution)/shard_map/psum | solution.py:61
  429.4 10.3 %psum.45 = f32[]{:T(128)} all-reduce(f32[]{:T(128)} %psum.44), channel_id=1, replica_groups=mesh['role'=2,'dp_0'=4,'dp_1'=4,'mp_0'=4,'mp_1'=2] {'dp_1'}, use_global_device_ids=true, to_apply=%region_16.0 | all-reduce | flops 1 | bytes 8 | tf_op jit(solution)/shard_map/psum | solution.py:61
  440.3 10.4 %psum.46 = f32[]{:T(128)} all-reduce(f32[]{:T(128)} %psum.45), channel_id=1, replica_groups=mesh['role'=2,'dp_0'=4,'dp_1'=4,'mp_0'=4,'mp_1'=2] {'mp_0'}, use_global_device_ids=true, to_apply=%region_17.0 | all-reduce | flops 1 | bytes 8 | tf_op jit(solution)/shard_map/psum | solution.py:61
  450.7 3.1 psum.47
  454.4 98.4 %all-reduce.7.cloned.1.call-done = bf16[1280,128]{1,0:T(8,128)(2,1)} async-done(((bf16[1280,128]{1,0:T(8,128)(2,1)}), bf16[1280,128]{1,0:T(8,128)(2,1)}) %all-reduce.7.cloned.1.call-update) | async-done | bytes 327696
  (102 shorter events, 30.6 us)
Async XLA Ops:
  8.0 13.7 %copy-start = (bf16[1568,160]{0,1:T(8,128)(2,1)S(1)}, bf16[1568,160]{0,1:T(8,128)(2,1)}, u32[]{:S(2)}) copy-start(bf16[1568,160]{0,1:T(8,128)(2,1)} %param.12) | copy-start | bytes 1505284
  9.5 25.1 %all-to-all-start = ((bf16[32,192,12]{1,2,0:T(8,128)(2,1)}), bf16[32,192,12]{1,2,0:T(8,128)(2,1)S(1)}, u32[]{:S(2)}, u32[]{:S(2)}) async-start(bf16[32,192,12]{1,2,0:T(8,128)(2,1)} %broadcast_in_dim.10), calls=%async_computation | async-start | bytes 524288 | tf_op jit(solution)/shard_map/all_to_all | solution.py:27
  22.6 13.2 %copy-start.10 = (bf16[512,160]{0,1:T(8,128)(2,1)}, bf16[512,160]{0,1:T(8,128)(2,1)S(1)}, u32[]{:S(2)}) copy-start(bf16[512,160]{0,1:T(8,128)(2,1)S(1)} %fusion.31) | copy-start | bytes 491524
  34.6 1.2 copy-start.12
  35.8 22.3 %copy-start.15 = (bf16[40,640]{1,0:T(8,128)(2,1)S(1)}, bf16[40,640]{1,0:T(8,128)(2,1)}, u32[]{:S(2)}) copy-start(bf16[40,640]{1,0:T(8,128)(2,1)} %param.14) | copy-start | bytes 153604
  35.8 22.2 %all-to-all-start.1 = ((bf16[8,512,160]{1,2,0:T(8,128)(2,1)}), bf16[8,512,160]{1,2,0:T(8,128)(2,1)S(1)}, u32[]{:S(2)}, u32[]{:S(2)}) async-start(bf16[8,512,160]{1,2,0:T(8,128)(2,1)} %broadcast_in_dim.11), calls=%async_computation.1 | async-start | bytes 2621440 | tf_op jit(solution)/shard_map/all_to_all | solution.py:27
  40.7 148.9 %all-gather.5.cloned.1.call-start = ((), (), s32[]{:S(2)}) async-start(), calls=%async_computation.9 | async-start | bytes 1689600 | tf_op jit(solution)/shard_map/all_gather | solution.py:153
  59.4 4.9 copy-start.16
  59.4 4.9 copy-start.17
  59.4 119.2 %copy-start.1 = (bf16[1024,384]{1,0:T(8,128)(2,1)S(1)}, bf16[1024,384]{1,0:T(8,128)(2,1)}, u32[]{:S(2)}) copy-start(bf16[1024,384]{1,0:T(8,128)(2,1)} %param.13) | copy-start | bytes 2359300
  59.4 125.5 %all-to-all-start.2 = ((bf16[32,40,640]{2,1,0:T(8,128)(2,1)}), bf16[32,40,640]{2,1,0:T(8,128)(2,1)}, u32[]{:S(2)}, u32[]{:S(2)}) async-start(bf16[32,40,640]{2,1,0:T(8,128)(2,1)} %stack.2), calls=%async_computation.2 | async-start | bytes 3276800 | tf_op jit(solution)/shard_map/all_to_all | solution.py:151
  64.2 185.8 %all-reduce.5.cloned.1.call-start = ((), (), s32[]{:S(2)}) async-start(), calls=%async_computation.8 | async-start | bytes 3145728 | tf_op jit(solution)/shard_map/psum | solution.py:196
  178.6 1.0 copy-start.8
  180.3 4.5 copy-start.4
  184.8 103.4 %reduce-scatter.3.cloned.1.call-start = ((), (), s32[]{:S(2)}) async-start(), calls=%async_computation.10 | async-start | bytes 2949120 | tf_op jit(solution)/shard_map/reduce_scatter | solution.py:166
  202.7 11.3 %all-to-all-start.4 = ((f32[16,1,1]{2,1,0:T(1,128)}), f32[16,1,1]{2,1,0:T(1,128)S(1)}, u32[]{:S(2)}, u32[]{:S(2)}) async-start(f32[16,1,1]{2,1,0:T(1,128)} %broadcast_in_dim.13), calls=%async_computation.5 | async-start | bytes 16384 | tf_op jit(solution)/shard_map/all_to_all | solution.py:27
  250.0 1.9 copy-start.2
  251.8 36.5 %copy-start.11 = (bf16[512,160]{0,1:T(8,128)(2,1)S(1)}, bf16[512,160]{0,1:T(8,128)(2,1)}, u32[]{:S(2)}) copy-start(bf16[512,160]{0,1:T(8,128)(2,1)} %copy-done.10) | copy-start | bytes 491524
  290.0 11.1 %all-to-all-start.3 = ((f32[8,1,1024]{2,1,0:T(1,128)}), f32[8,1,1024]{2,1,0:T(1,128)S(1)}, u32[]{:S(2)}, u32[]{:S(2)}) async-start(f32[8,1,1024]{2,1,0:T(1,128)} %broadcast_in_dim.12), calls=%async_computation.4 | async-start | bytes 65536 | tf_op jit(solution)/shard_map/all_to_all | solution.py:27
  297.1 55.7 %reduce-scatter.5.cloned.1.call-start = ((), (), s32[]{:S(2)}) async-start(), calls=%async_computation.11 | async-start | bytes 1769472 | tf_op jit(solution)/shard_map/reduce_scatter | solution.py:71
  302.2 11.2 %copy-start.9 = (bf16[384,352]{1,0:T(8,128)(2,1)S(1)}, bf16[384,352]{1,0:T(8,128)(2,1)}, u32[]{:S(2)}) copy-start(bf16[384,352]{1,0:T(8,128)(2,1)} %reshape.201) | copy-start | bytes 811012
  302.2 11.2 %collective-permute-start = (bf16[512,160]{0,1:T(8,128)(2,1)S(1)}, bf16[512,160]{0,1:T(8,128)(2,1)S(1)}, u32[]{:S(2)}, u32[]{:S(2)}) collective-permute-start(bf16[512,160]{0,1:T(8,128)(2,1)S(1)} %multiply_convert_fusion.2), channel_id=1, source_target_pairs={{0,128},{1,129},{2,130},{3,131},{4,132},{5,133},{6,134},{7,135},{8... | collective-permute-start | bytes 491528 | tf_op jit(solution)/shard_map/ppermute | solution.py:50
  310.3 4.5 copy-start.7
  316.6 65.2 %all-gather.7.cloned.1.call-start = ((), (), s32[]{:S(2)}) async-start(), calls=%async_computation.12 | async-start | bytes 1769472 | tf_op jit(solution)/shard_map/all_gather | solution.py:74
  381.8 2.3 copy-start.3
  384.0 1.8 copy-start.5
  384.9 0.9 copy-start.13
  385.9 1.1 copy-start.6
  385.9 1.2 copy-start.14
  390.2 38.6 %copy-start.18 = (u32[256]{0:T(256)S(1)}, u32[256]{0:T(256)}, u32[]{:S(2)}) copy-start(u32[256]{0:T(256)} %constant.79) | copy-start | bytes 3076
  390.2 165.5 %all-to-all-start.5 = ((f32[32,192,12]{1,2,0:T(8,128)}), f32[32,192,12]{1,2,0:T(8,128)S(1)}, u32[]{:S(2)}, u32[]{:S(2)}) async-start(f32[32,192,12]{1,2,0:T(8,128)} %bitcast.10), calls=%async_computation.7 | async-start | bytes 1048576 | tf_op jit(solution)/shard_map/all_to_all | solution.py:99
  400.2 152.7 %all-reduce.7.cloned.1.call-start = ((), (), s32[]{:S(2)}) async-start(), calls=%async_computation.13 | async-start | bytes 655360
Sparse Core Ops, SparseCore 0:
  43.3 146.2 all-gather.4
  404.4 148.3 all-reduce.6
Sparse Core Ops, SparseCore 1:
  184.9 65.0 all-reduce.4
  252.4 35.8 reduce-scatter.2
  316.7 36.0 reduce-scatter.4
  354.6 27.1 all-gather.6
